TPU v7x, 8 devices: a whole 2x2x1 slice. The times are simulated.
8 devices in a mesh: data: 1 (over z), col: 2 (over y), row: 4 (over x, core).
Axes of the slice: x: 2, y: 2, z: 1, core: 2. Of those that a mesh axis runs over, the one named last changes fastest.
Arguments:
- image: bfloat16 [256, 128, 3], P(('data', 'row'), 'col')
- w_enc1a: bfloat16 [3, 3, 3, 192], replicated
- b_enc1a: float32 [192], replicated
- w_enc1b: bfloat16 [3, 3, 192, 192], replicated
- b_enc1b: float32 [192], replicated
- w_enc2a: bfloat16 [3, 3, 192, 384], replicated
- b_enc2a: float32 [384], replicated
- w_enc2b: bfloat16 [3, 3, 384, 384], replicated
- b_enc2b: float32 [384], replicated
- w_mid_a: bfloat16 [3, 3, 384, 768], replicated
- b_mid_a: float32 [768], replicated
- w_mid_b: bfloat16 [3, 3, 768, 768], replicated
- b_mid_b: float32 [768], replicated
- w_up2: bfloat16 [2, 2, 768, 384], replicated
- w_dec2a: bfloat16 [3, 3, 768, 384], replicated
- b_dec2a: float32 [384], replicated
- w_dec2b: bfloat16 [3, 3, 384, 384], replicated
- b_dec2b: float32 [384], replicated
- w_up1: bfloat16 [2, 2, 384, 192], replicated
- w_dec1a: bfloat16 [3, 3, 384, 192], replicated
- b_dec1a: float32 [192], replicated
- w_dec1b: bfloat16 [3, 3, 192, 192], replicated
- b_dec1b: float32 [192], replicated
- w_head: bfloat16 [192, 6], replicated
- b_head: float32 [6], replicated
Outputs:
- output: float32 [256, 128, 6], P(('data', 'row'), 'col')
All inputs are finite; a program needn't handle non-finite values.
Results may differ from a plain program's by a relative error of at most 0.0168.
Values are sent between devices in bfloat16 or wider.
A program may use at most 1 GiB of HBM per device.

v0:
```python
import functools

import jax
import jax.numpy as jnp
import numpy as np
from jax import lax
from jax.experimental import pallas as pl
from jax.experimental.pallas import tpu as pltpu
from jax.sharding import PartitionSpec as P

MESH = pl.DeviceIdType.MESH
F32 = jnp.float32
BF16 = jnp.bfloat16
ROWS = 18
SIDE = 16
PIX = SIDE * SIDE
EXCHANGE_FACTOR = (2, 2, 1, 1, 2, 2, 4, 4)
EXCHANGE_LANES = (256, 384, 384, 768, 768, 384, 384, 256)


def kernel(row_count, x8, w8, we1b, we2a, we2b, wma, wmb, wu2, wd2a, wd2b, wu1, wd1a, wd1b, wh,
           be1a, be1b, be2a, be2b, bma, bmb, bd2a, bd2b, bd1a, bd1b, bh, y,
           vw8, ve1b, ve2a, ve2b, vma, vmb, vu2, vd2a, vd2b, vu1, vd1a, vd1b,
           h1, cat1, d1a, p1, e2a, cat2, d2, p2, ma, mid,
           sc0, sc1, sc2, sc3, sc4, sc5, sc6, sc7, rc0, rc1, rc2, rc3, rc4, rc5, rc6, rc7,
           w_sem, send_sem, recv_sem):
    row = lax.axis_index("row")
    col = lax.axis_index("col")
    data = lax.axis_index("data")
    last = row_count - 1
    has_up = row > 0
    has_down = row < last
    up = (data, col, row - 1)
    down = (data, col, row + 1)
    side = (data, 1 - col, row)
    side_up = (data, 1 - col, row - 1)
    side_down = (data, 1 - col, row + 1)
    edge = (1 - col) * (SIDE - 1)
    send_cols = (sc0, sc1, sc2, sc3, sc4, sc5, sc6, sc7)
    recv_cols = (rc0, rc1, rc2, rc3, rc4, rc5, rc6, rc7)

    loads = (
        (w8, vw8), (we1b, ve1b), (we2a, ve2a.at[:, :, 64:256, :]), (we2b, ve2b), (wma, vma), (wmb, vmb),
        (wu2, vu2), (wd2a, vd2a), (wd2b, vd2b), (wu1, vu1), (wd1a, vd1a), (wd1b, vd1b.at[:, :, 0:192, :]),
    )
    copies = [pltpu.make_async_copy(src, dst, w_sem.at[k]) for k, (src, dst) in enumerate(loads)]
    for k in range(4):
        copies[k].start()

    def zero_halo(buf, factor):
        shape = buf.shape[1:2] + buf.shape[3:]
        buf[0, :, ROWS - 1] = jnp.zeros(shape, BF16)
        buf[factor - 1, :, 0] = jnp.zeros(shape, BF16)

    for buf, factor in ((h1, 4), (cat1, 4), (p1, 2), (e2a, 2), (cat2, 2), (p2, 1), (ma, 1)):
        zero_halo(buf, factor)

    def zero_plane(t, carry):
        d1a[t // 6, lax.rem(t, 6)] = jnp.zeros(d1a.shape[2:], BF16)
        return carry

    lax.fori_loop(0, 24, zero_plane, 0)
    for buf, factor in zip(recv_cols, EXCHANGE_FACTOR):
        buf[factor:factor + 2] = jnp.zeros((2,) + buf.shape[1:], BF16)
    ve2a[:, :, 0:64, :] = jnp.zeros((3, 3, 64, 384), BF16)
    vd1b[:, :, 192:256, :] = jnp.zeros((3, 3, 64, 192), BF16)

    barrier = pltpu.get_barrier_semaphore()
    pl.semaphore_signal(barrier, inc=1, device_id=side, device_id_type=MESH)

    @pl.when(has_up)
    def _():
        pl.semaphore_signal(barrier, inc=1, device_id=up, device_id_type=MESH)
        pl.semaphore_signal(barrier, inc=1, device_id=side_up, device_id_type=MESH)

    @pl.when(has_down)
    def _():
        pl.semaphore_signal(barrier, inc=1, device_id=down, device_id_type=MESH)
        pl.semaphore_signal(barrier, inc=1, device_id=side_down, device_id_type=MESH)

    for k in range(4, len(copies)):
        copies[k].start()

    def relu_bias(acc, bias):
        return jnp.maximum(acc + bias[...], 0.0)

    copies[0].wait()
    ext = ROWS * SIDE
    pos = lax.broadcasted_iota(jnp.int32, (ext, 256), 0)
    pos_row = pos // SIDE
    pos_col = lax.rem(pos, SIDE)
    off_rows = ((pos_row == 0) & (row == 0)) | ((pos_row == ROWS - 1) & (row == last))
    off_left = off_rows | ((pos_col == 0) & (col == 0))
    off_right = off_rows | ((pos_col == SIDE - 1) & (col == 1))

    def first_conv(a, carry):
        for b in range(6):
            acc = jnp.dot(x8[...], vw8[a * 6 + b], preferred_element_type=F32)
            off = off_left if b == 0 else off_right if b == 5 else off_rows
            out = jnp.where(off, 0.0, relu_bias(acc, be1a)).astype(BF16)
            h1[a, b] = out.reshape(ROWS, SIDE, 256)
        return carry

    lax.fori_loop(0, 4, first_conv, 0)

    def taps(buf, factor, a):
        rows = []
        for b in range(factor):
            parts = []
            for dy in range(3):
                shifted = a + (dy - 1) + factor
                plane = lax.rem(shifted, factor)
                start = shifted // factor
                for dx in range(3):
                    piece = buf[plane, b + dx, pl.ds(start, SIDE)]
                    parts.append(piece.reshape(PIX, piece.shape[-1]))
            rows.append(jnp.concatenate(parts, axis=1))
        return rows[0] if factor == 1 else jnp.concatenate(rows, axis=0)

    def conv(buf, factor, a, weight, bias, transposed=False):
        lhs = taps(buf, factor, a)
        if transposed:
            acc = None
            width = weight.shape[-1]
            for t in range(9):
                part = lax.dot_general(lhs[:, t * width:(t + 1) * width], weight[t // 3, t % 3],
                                       (((1,), (1,)), ((), ())), preferred_element_type=F32)
                acc = part if acc is None else acc + part
        else:
            flat = weight[...].reshape(lhs.shape[1], weight.shape[-1])
            acc = jnp.dot(lhs, flat, preferred_element_type=F32)
        return relu_bias(acc, bias).astype(BF16)

    def store_row(buf, factor, a, value, lane, width):
        for b in range(factor):
            buf[a, b + 1, 1:ROWS - 1, :, lane:lane + width] = value[b * PIX:(b + 1) * PIX].reshape(SIDE, SIDE, width)

    def conv_layer(src, dst, factor, weight, bias, lane, transposed=False):
        width = bias.shape[-1]

        def body(a, carry):
            store_row(dst, factor, a, conv(src, factor, a, weight, bias, transposed), lane, width)
            return carry

        if factor == 1:
            body(0, 0)
        else:
            lax.fori_loop(0, factor, body, 0)

    def pool(src, dst, factor, lane, width):
        for a in range(factor):
            for b in range(factor):
                best = None
                for p in range(2):
                    for q in range(2):
                        piece = src[2 * a + p, 2 * b + q + 1, 1:ROWS - 1, :, lane:lane + width]
                        best = piece if best is None else jnp.maximum(best, piece)
                dst[a, b + 1, 1:ROWS - 1] = best

    def messages(index, buf):
        factor = EXCHANGE_FACTOR[index]
        cols, got = send_cols[index], recv_cols[index]

        def remote(src, dst, k, device):
            return pltpu.make_async_remote_copy(
                src_ref=src, dst_ref=dst, send_sem=send_sem.at[index, k], recv_sem=recv_sem.at[index, k],
                device_id=device, device_id_type=MESH)

        to_side = remote(cols, got.at[pl.ds(0, factor)], 0, side)
        to_up = remote(buf.at[0, :, 1], buf.at[0, :, ROWS - 1], 1, up)
        to_down = remote(buf.at[factor - 1, :, ROWS - 2], buf.at[factor - 1, :, 0], 2, down)
        to_side_up = remote(cols.at[0], got.at[factor + 1], 3, side_up)
        to_side_down = remote(cols.at[factor - 1], got.at[factor], 4, side_down)
        return to_side, to_up, to_down, to_side_up, to_side_down

    def exchange(index, buf):
        factor = EXCHANGE_FACTOR[index]
        lanes = EXCHANGE_LANES[index]
        cols, got = send_cols[index], recv_cols[index]
        at = lax.broadcasted_iota(jnp.int32, (PIX, lanes), 0)
        at_col = lax.rem(at, SIDE)

        def shifted_planes(a, carry):
            left = buf[a, factor, 1:ROWS - 1].reshape(PIX, lanes).astype(F32)
            left = jnp.where(at_col == 0, 0.0, pltpu.roll(left, 1, 0))
            buf[a, 0, 1:ROWS - 1] = left.astype(BF16).reshape(SIDE, SIDE, lanes)
            right = buf[a, 1, 1:ROWS - 1].reshape(PIX, lanes).astype(F32)
            right = jnp.where(at_col == SIDE - 1, 0.0, pltpu.roll(right, PIX - 1, 0))
            buf[a, factor + 1, 1:ROWS - 1] = right.astype(BF16).reshape(SIDE, SIDE, lanes)
            return carry

        lax.fori_loop(0, factor, shifted_planes, 0)
        pick_row = lax.broadcasted_iota(jnp.int32, (SIDE, PIX), 0)
        pick_at = lax.broadcasted_iota(jnp.int32, (SIDE, PIX), 1)
        pick = (pick_at == pick_row * SIDE + edge).astype(F32).astype(BF16)
        for a in range(factor):
            plane = buf[a, 1 + (factor - 1) * (1 - col), 1:ROWS - 1].reshape(PIX, lanes)
            cols[a] = jnp.dot(pick, plane, preferred_element_type=F32).astype(BF16)
        to_side, to_up, to_down, to_side_up, to_side_down = messages(index, buf)
        to_side.start()

        @pl.when(has_up)
        def _():
            to_up.start()
            to_side_up.start()

        @pl.when(has_down)
        def _():
            to_down.start()
            to_side_down.start()

        to_side.wait()

        @pl.when(has_up)
        def _():
            to_up.wait_send()
            to_side_up.wait_send()
            to_down.wait_recv()
            to_side_down.wait_recv()

        @pl.when(has_down)
        def _():
            to_down.wait_send()
            to_side_down.wait_send()
            to_up.wait_recv()
            to_side_up.wait_recv()

        place_at = lax.broadcasted_iota(jnp.int32, (ROWS * SIDE, 3 * SIDE), 0)
        place_from = lax.broadcasted_iota(jnp.int32, (ROWS * SIDE, 3 * SIDE), 1)
        place = (lax.rem(place_at, SIDE) == edge) & (place_at // SIDE + SIDE - 1 == place_from)
        place = place.astype(F32).astype(BF16)
        fix = (factor + 1) * (1 - col)

        def insert(a, carry):
            halo = jnp.concatenate([got[factor], got[a], got[factor + 1]], axis=0)
            put = jnp.dot(place, halo, preferred_element_type=F32)
            plane = buf[a, fix].reshape(ROWS * SIDE, lanes).astype(F32)
            buf[a, fix] = (plane + put).astype(BF16).reshape(ROWS, SIDE, lanes)
            return carry

        lax.fori_loop(0, factor, insert, 0)

    copies[1].wait()
    conv_layer(h1, cat1, 4, ve1b, be1b, 128)
    pool(cat1, p1, 2, 128, 256)

    total = jnp.where(has_up, 2, 0) + jnp.where(has_down, 2, 0) + 1
    pl.semaphore_wait(barrier, total)
    exchange(0, p1)
    copies[2].wait()
    conv_layer(p1, e2a, 2, ve2a, be2a, 0)
    exchange(1, e2a)
    copies[3].wait()
    conv_layer(e2a, cat2, 2, ve2b, be2b, 384)
    pool(cat2, p2, 1, 384, 384)
    exchange(2, p2)
    copies[4].wait()
    conv_layer(p2, ma, 1, vma, bma, 0)
    exchange(3, ma)
    copies[5].wait()
    mid[...] = conv(ma, 1, 0, vmb, bmb)
    copies[6].wait()
    for p in range(2):
        for q in range(2):
            out = jnp.dot(mid[...], vu2[p, q], preferred_element_type=F32).astype(BF16)
            cat2[p, q + 1, 1:ROWS - 1, :, 0:384] = out.reshape(SIDE, SIDE, 384)
    exchange(4, cat2)
    copies[7].wait()
    conv_layer(cat2, e2a, 2, vd2a, bd2a, 0)
    exchange(5, e2a)
    copies[8].wait()

    def dec2b(a, carry):
        d2[pl.ds(2 * a * PIX, 2 * PIX)] = conv(e2a, 2, a, vd2b, bd2b)
        return carry

    lax.fori_loop(0, 2, dec2b, 0)
    copies[9].wait()

    def up1(t, carry):
        a = t // 2
        p = lax.rem(t, 2)
        lhs = d2[pl.ds(2 * a * PIX, 2 * PIX)]
        for q in range(2):
            out = lax.dot_general(lhs, vu1[p, q], (((1,), (1,)), ((), ())), preferred_element_type=F32).astype(BF16)
            for b in range(2):
                cat1[t, 2 * b + q + 1, 1:ROWS - 1, :, 0:192] = out[b * PIX:(b + 1) * PIX].reshape(SIDE, SIDE, 192)
        return carry

    lax.fori_loop(0, 4, up1, 0)
    exchange(6, cat1)
    copies[10].wait()
    conv_layer(cat1, d1a, 4, vd1a, bd1a, 0, transposed=True)
    exchange(7, d1a)
    copies[11].wait()

    def dec1b(a, carry):
        out = conv(d1a, 4, a, vd1b, bd1b)
        for b in range(4):
            head = lax.dot_general(wh[...], out[b * PIX:(b + 1) * PIX], (((1,), (1,)), ((), ())), preferred_element_type=F32)
            y[a, b] = head + bh[...]
        return carry

    lax.fori_loop(0, 4, dec1b, 0)


def solution(mesh):
    row_count = mesh.shape["row"]
    col_count = mesh.shape["col"]
    row_next = [(source, source + 1) for source in range(row_count - 1)]
    row_prev = [(source + 1, source) for source in range(row_count - 1)]
    col_next = [(source, source + 1) for source in range(col_count - 1)]
    col_prev = [(source + 1, source) for source in range(col_count - 1)]
    tile_spec = P(("data", "row"), "col", None)

    def with_halo(tile, depth):
        from_above = lax.ppermute(tile[-depth:], "row", row_next)
        from_below = lax.ppermute(tile[:depth], "row", row_prev)
        tall_tile = jnp.concatenate([from_above, tile, from_below], axis=0)
        from_left = lax.ppermute(tall_tile[:, -depth:], "col", col_next)
        from_right = lax.ppermute(tall_tile[:, :depth], "col", col_prev)
        return jnp.concatenate([from_left, tall_tile, from_right], axis=1)

    def patches(image_tile):
        haloed = with_halo(image_tile, 2)
        padded = jnp.pad(haloed, ((3, 5), (0, 0), (0, 0)))
        select = np.zeros((68, 8, 16), np.float32)
        for px in range(8):
            for j in range(16):
                select[4 * j + px, px, j] = 1.0
        picked = jnp.einsum("rwc,wpj->rpjc", padded, jnp.asarray(select, BF16), preferred_element_type=F32).astype(BF16)
        blocks = picked.reshape(19, 4, 8, 16, 3)
        rows = jnp.concatenate([blocks[:18], blocks[1:, :2]], axis=1)
        return rows.transpose(0, 3, 1, 2, 4).reshape(288, 144)

    def first_weights(w_enc1a):
        planes = []
        for a in range(4):
            for b in range(6):
                planes.append(jnp.pad(w_enc1a, ((a, 3 - a), (b, 5 - b), (0, 0), (0, 64))))
        return jnp.stack(planes).reshape(24, 144, 256)

    def device_body(image_tile, *params):
        (w_enc1a, b_enc1a, w_enc1b, b_enc1b, w_enc2a, b_enc2a, w_enc2b, b_enc2b,
         w_mid_a, b_mid_a, w_mid_b, b_mid_b, w_up2, w_dec2a, b_dec2a, w_dec2b, b_dec2b,
         w_up1, w_dec1a, b_dec1a, w_dec1b, b_dec1b, w_head, b_head) = params
        anywhere = pl.BlockSpec(memory_space=pl.ANY)
        vmem = pl.BlockSpec(memory_space=pltpu.VMEM)
        operands = [
            patches(image_tile), first_weights(w_enc1a),
            jnp.pad(w_enc1b, ((0, 0), (0, 0), (0, 64), (64, 0))), w_enc2a, w_enc2b, w_mid_a, w_mid_b,
            w_up2, w_dec2a, w_dec2b, jnp.swapaxes(w_up1, 2, 3), jnp.swapaxes(w_dec1a, 2, 3), w_dec1b, w_head.T,
            jnp.pad(b_enc1a, (0, 64))[None], jnp.pad(b_enc1b, (64, 0))[None], b_enc2a[None], b_enc2b[None],
            b_mid_a[None], b_mid_b[None], b_dec2a[None], b_dec2b[None], b_dec1a[None], b_dec1b[None], b_head[:, None],
        ]
        specs = [vmem] + [anywhere] * 12 + [vmem] * 12
        level = lambda factor, lanes: pltpu.VMEM((factor, factor + 2, ROWS, SIDE, lanes), BF16)
        scratch = [
            pltpu.VMEM((24, 144, 256), BF16), pltpu.VMEM((3, 3, 256, 256), BF16), pltpu.VMEM((3, 3, 256, 384), BF16),
            pltpu.VMEM((3, 3, 384, 384), BF16), pltpu.VMEM((3, 3, 384, 768), BF16), pltpu.VMEM((3, 3, 768, 768), BF16),
            pltpu.VMEM((2, 2, 768, 384), BF16), pltpu.VMEM((3, 3, 768, 384), BF16), pltpu.VMEM((3, 3, 384, 384), BF16),
            pltpu.VMEM((2, 2, 192, 384), BF16), pltpu.VMEM((3, 3, 192, 384), BF16), pltpu.VMEM((3, 3, 256, 192), BF16),
            level(4, 256), level(4, 384), level(4, 256), level(2, 256), level(2, 384), level(2, 768),
            pltpu.VMEM((4 * PIX, 384), BF16), level(1, 384), level(1, 768), pltpu.VMEM((PIX, 768), BF16),
        ]
        scratch += [pltpu.VMEM((f, SIDE, c), BF16) for f, c in zip(EXCHANGE_FACTOR, EXCHANGE_LANES)]
        scratch += [pltpu.VMEM((f + 2, SIDE, c), BF16) for f, c in zip(EXCHANGE_FACTOR, EXCHANGE_LANES)]
        scratch += [pltpu.SemaphoreType.DMA((12,)), pltpu.SemaphoreType.DMA((8, 5)), pltpu.SemaphoreType.DMA((8, 5))]
        out = pl.pallas_call(
            functools.partial(kernel, row_count),
            name="unet",
            out_shape=jax.ShapeDtypeStruct((4, 4, 6, PIX), F32),
            in_specs=specs,
            out_specs=vmem,
            scratch_shapes=scratch,
            compiler_params=pltpu.CompilerParams(collective_id=0, has_side_effects=True, vmem_limit_bytes=67043328),
        )(*operands)
        grid = out.reshape(4, 4, 6, 16, 16).transpose(3, 0, 4, 1, 2)
        return grid.reshape(64, 64, 6)

    def program(image, *params):
        mapped = jax.shard_map(device_body, mesh=mesh, in_specs=(tile_spec,) + tuple([P()] * len(params)), out_specs=tile_spec, check_vma=False)
        return mapped(image, *params)

    return program
```

profile of v0, /device:TPU:0, one launch (start us, length us, event | category | flops | bytes accessed | tf_op | source)
XLA Modules:
  0.0 157.8 jit_solution(18235739860704511148)
XLA Ops:
  1.5 3.4 %collective-permute-start = (bf16[2,64,3]{0,1,2:T(8,128)(2,1)}, bf16[2,64,3]{0,1,2:T(8,128)(2,1)}, u32[]{:S(2)}, u32[]{:S(2)}) collective-permute-start(bf16[2,64,3]{0,1,2:T(8,128)(2,1)} %copy.34), channel_id=1, source_target_pairs={{0,1},{1,2},{2,3},{4,5},{5,6},{6,7}} | collective-permute-start | bytes 2312 | tf_op jit(solution)/shard_map/ppermute | solution.py:317
  5.6 1.3 collective-permute-start.1
  6.9 1.9 %fusion.26 = (bf16[6,8,3,256]{3,2,1,0:T(4,128)(2,1)}, bf16[6,8,3,256]{3,2,1,0:T(4,128)(2,1)}, bf16[6,8,3,256]{3,2,1,0:T(4,128)(2,1)}, bf16[6,8,3,256]{3,2,1,0:T(...) fusion(bf16[3,3,3,192]{3,2,1,0:T(4,128)(2,1)} %param.27), kind=kLoop, calls=%fused_computation.54 | loop fusion | bytes 452736 | tf_op jit(solution)/shard_map/jit(_pad)/pad | solution.py:340
  8.8 1.5 fusion.25
  10.3 1.5 fusion.24
  13.3 1.6 %stack.76 = bf16[1,144,256]{2,1,0:T(8,128)(2,1)} reshape(bf16[6,8,3,256]{3,2,1,0:T(4,128)(2,1)} %get-tuple-element.31) | data formatting | bytes 147456 | tf_op jit(solution)/shard_map/stack | solution.py:341
  14.9 1.6 stack.77
  16.5 1.6 stack.78
  18.1 1.6 %stack.79 = bf16[1,144,256]{2,1,0:T(8,128)(2,1)} reshape(bf16[6,8,3,256]{3,2,1,0:T(4,128)(2,1)} %get-tuple-element.28) | data formatting | bytes 147456 | tf_op jit(solution)/shard_map/stack | solution.py:341
  19.7 1.6 %stack.80 = bf16[1,144,256]{2,1,0:T(8,128)(2,1)} reshape(bf16[6,8,3,256]{3,2,1,0:T(4,128)(2,1)} %get-tuple-element.27) | data formatting | bytes 147456 | tf_op jit(solution)/shard_map/stack | solution.py:341
  26.5 1.0 constant_dynamic-update-slice_fusion.21
  36.6 1.3 copy.41.bh
  39.9 4.2 %collective-permute-start.2 = (bf16[68,2,3]{0,1,2:T(2,128)(2,1)S(1)}, bf16[68,2,3]{0,1,2:T(2,128)(2,1)S(1)}, u32[]{:S(2)}, u32[]{:S(2)}) collective-permute-start(bf16[68,2,3]{0,1,2:T(2,128)(2,1)S(1)} %get-tuple-element.5), channel_id=1, source_target_pairs={{0,4},{1,5},{2,6},{3,7}} | collective-permute-start | bytes 2456 | tf_op jit(solution)/shard_map/ppermute | solution.py:320
  44.2 1.3 collective-permute-start.3
  46.7 1.3 broadcast_in_dim.39.bd2a
  48.0 1.3 broadcast_in_dim.40.bd2b
  49.2 1.3 pad.138
  50.5 1.3 pad.139
  51.8 1.4 pad.137.we1b
  53.2 1.1 fusion
  56.6 93.5 %unet.1 = f32[4,4,6,256]{3,2,1,0:T(8,128)} custom-call(bf16[288,144]{1,0:T(8,128)(2,1)} %copy.40.x8, bf16[24,144,256]{2,1,0:T(8,128)(2,1)} %copy-done, bf16[3,3,256,256]{3,2,1,0:T(8,128)(2,1)} %pad.137.we1b, bf16[3,3,192,384]{3,2,1,0:T(8,128)(2,1)} %we2a.1, bf16[3,3,384,384]{3,2,1,0:T(8,128)(2,1)} %we2b.1, bf16[3,3,384,768]{3,2,1,0:T(8,128)(2,1)} %wma.1, ...), custom_call_target="tpu_custom_call" | custom-call | tf_op jit(solution)/shard_map/unet/pallas_call | solution.py:369
  151.1 1.2 reshape.64
  152.3 3.4 %copy.43 = f32[16,4,16,4,6]{3,2,1,0,4:T(8,128)S(1)} copy(f32[16,4,16,4,6]{2,0,3,4,1:T(8,128)} %bitcast.31) | data formatting | bytes 196608 | tf_op jit(solution)/shard_map/transpose | solution.py:378
  155.7 2.1 %reshape.65 = f32[64,64,6]{1,0,2:T(8,128)} reshape(f32[16,4,16,4,6]{3,2,1,0,4:T(8,128)S(1)} %copy.43) | data formatting | bytes 196608 | tf_op jit(solution)/shard_map/reshape | solution.py:379
  (79 shorter events, 24.4 us)
Async XLA Ops:
  1.5 37.7 %collective-permute-start = (bf16[2,64,3]{0,1,2:T(8,128)(2,1)}, bf16[2,64,3]{0,1,2:T(8,128)(2,1)}, u32[]{:S(2)}, u32[]{:S(2)}) collective-permute-start(bf16[2,64,3]{0,1,2:T(8,128)(2,1)} %copy.34), channel_id=1, source_target_pairs={{0,1},{1,2},{2,3},{4,5},{5,6},{6,7}} | collective-permute-start | bytes 2312 | tf_op jit(solution)/shard_map/ppermute | solution.py:317
  5.6 33.5 %collective-permute-start.1 = (bf16[2,64,3]{0,1,2:T(8,128)(2,1)}, bf16[2,64,3]{0,1,2:T(8,128)(2,1)}, u32[]{:S(2)}, u32[]{:S(2)}) collective-permute-start(bf16[2,64,3]{0,1,2:T(8,128)(2,1)} %copy.35), channel_id=1, source_target_pairs={{1,0},{2,1},{3,2},{5,4},{6,5},{7,6}} | collective-permute-start | bytes 2312 | tf_op jit(solution)/shard_map/ppermute | solution.py:318
  25.5 0.9 copy-start.2
  26.4 11.5 %copy-start.3 = (f32[768]{0:T(1024)S(1)}, f32[768]{0:T(1024)}, u32[]{:S(2)}) copy-start(f32[768]{0:T(1024)} %param.36) | copy-start | bytes 9220
  26.4 12.1 %copy-start.4 = (f32[768]{0:T(1024)S(1)}, f32[768]{0:T(1024)}, u32[]{:S(2)}) copy-start(f32[768]{0:T(1024)} %param.38) | copy-start | bytes 9220
  26.4 19.1 %copy-start.5 = (f32[384]{0:T(512)S(1)}, f32[384]{0:T(512)}, u32[]{:S(2)}) copy-start(f32[384]{0:T(512)} %param.32) | copy-start | bytes 4612
  26.5 19.6 %copy-start.6 = (f32[384]{0:T(512)S(1)}, f32[384]{0:T(512)}, u32[]{:S(2)}) copy-start(f32[384]{0:T(512)} %param.34) | copy-start | bytes 4612
  26.5 25.4 %copy-start.1 = (bf16[3,3,192,192]{3,2,1,0:T(8,128)(2,1)S(1)}, bf16[3,3,192,192]{3,2,1,0:T(8,128)(2,1)}, u32[]{:S(2)}) copy-start(bf16[3,3,192,192]{3,2,1,0:T(8,128)(2,1)} %param.29) | copy-start | bytes 1990660
  35.5 17.7 %copy-start.7 = (bf16[68,8,16,1]{0,2,1,3:T(8,128)(2,1)S(1)}, bf16[68,8,16,1]{0,2,1,3:T(8,128)(2,1)}, u32[]{:S(2)}) copy-start(bf16[68,8,16,1]{0,2,1,3:T(8,128)(2,1)} %constant.64) | copy-start | bytes 52228
  35.6 19.0 %copy-start = (bf16[24,144,256]{2,1,0:T(8,128)(2,1)}, bf16[24,144,256]{2,1,0:T(8,128)(2,1)S(1)}, u32[]{:S(2)}) copy-start(bf16[24,144,256]{2,1,0:T(8,128)(2,1)S(1)} %constant_dynamic-update-slice_fusion.w8) | copy-start | bytes 5308420
  39.9 13.3 %collective-permute-start.2 = (bf16[68,2,3]{0,1,2:T(2,128)(2,1)S(1)}, bf16[68,2,3]{0,1,2:T(2,128)(2,1)S(1)}, u32[]{:S(2)}, u32[]{:S(2)}) collective-permute-start(bf16[68,2,3]{0,1,2:T(2,128)(2,1)S(1)} %get-tuple-element.5), channel_id=1, source_target_pairs={{0,4},{1,5},{2,6},{3,7}} | collective-permute-start | bytes 2456 | tf_op jit(solution)/shard_map/ppermute | solution.py:320
  44.2 9.0 %collective-permute-start.3 = (bf16[68,2,3]{0,1,2:T(2,128)(2,1)S(1)}, bf16[68,2,3]{0,1,2:T(2,128)(2,1)S(1)}, u32[]{:S(2)}, u32[]{:S(2)}) collective-permute-start(bf16[68,2,3]{0,1,2:T(2,128)(2,1)S(1)} %get-tuple-element.6), channel_id=1, source_target_pairs={{4,0},{5,1},{6,2},{7,3}} | collective-permute-start | bytes 2456 | tf_op jit(solution)/shard_map/ppermute | solution.py:321
where the time goes:
time: 159 us; the launch traced here: 158 us
  Pallas kernels  93.5 us (59%)
  local copies, waits for them, and re-layouts  51.7 us (33%)
  starting transfers between devices  10.2 us (6%)
    pallas_call x1, Pallas kernels, device_body(): pl.pallas_call(functools.partial(kernel, row_count), name='unet', out_sha...  93.5 us
    another operation x25, local copies, waits for them, and re-layouts, first_weights(): return jnp.stack(planes).reshape(24, 144, 256)  13.6 us
    unnamed x40, local copies, waits for them, and re-layouts  11.1 us
    pad x3, local copies, waits for them, and re-layouts, first_weights(): planes.append(jnp.pad(w_enc1a, ((a, 3 - a), (b, 5 - b), (0, 0), (0, 64))))  4.86 us
    ppermute x1, starting transfers between devices, with_halo(): from_left = lax.ppermute(tall_tile[:, -depth:], 'col', col_next)  4.24 us
    ppermute x1, starting transfers between devices, with_halo(): from_above = lax.ppermute(tile[-depth:], 'row', row_next)  3.37 us
    transpose x1, local copies, waits for them, and re-layouts, device_body(): grid = out.reshape(4, 4, 6, 16, 16).transpose(3, 0, 4, 1, 2)  3.37 us
  transfers between devices with their start and end apart: 4, of which 0 were waited for; matrix products, arithmetic and copies ran while one was open for 26% of the time, Pallas kernels for 0%

commit v1 on v0

--- a/solution.py
+++ b/solution.py
@@ -2,7 +2,6 @@
 
 import jax
 import jax.numpy as jnp
-import numpy as np
 from jax import lax
 from jax.experimental import pallas as pl
 from jax.experimental.pallas import tpu as pltpu
@@ -14,15 +13,16 @@
 ROWS = 18
 SIDE = 16
 PIX = SIDE * SIDE
-EXCHANGE_FACTOR = (2, 2, 1, 1, 2, 2, 4, 4)
-EXCHANGE_LANES = (256, 384, 384, 768, 768, 384, 384, 256)
-
-
-def kernel(row_count, x8, w8, we1b, we2a, we2b, wma, wmb, wu2, wd2a, wd2b, wu1, wd1a, wd1b, wh,
+EXCHANGE_FACTOR = (2, 2, 1, 1, 2, 2, 4, 4, 1)
+EXCHANGE_LANES = (256, 384, 384, 768, 768, 384, 384, 256, 128)
+PATCH = 192
+
+
+def kernel(row_count, x, we1a, we1b, we2a, we2b, wma, wmb, wu2, wd2a, wd2b, wu1, wd1a, wd1b, wh,
            be1a, be1b, be2a, be2b, bma, bmb, bd2a, bd2b, bd1a, bd1b, bh, y,
-           vw8, ve1b, ve2a, ve2b, vma, vmb, vu2, vd2a, vd2b, vu1, vd1a, vd1b,
-           h1, cat1, d1a, p1, e2a, cat2, d2, p2, ma, mid,
-           sc0, sc1, sc2, sc3, sc4, sc5, sc6, sc7, rc0, rc1, rc2, rc3, rc4, rc5, rc6, rc7,
+           vw8, re1b, ve1b, ve2a, ve2b, vma, vmb, vu2, vd2a, vd2b, vu1, vd1a, vd1b,
+           h1, cat1, d1a, p1, e2a, cat2, d2, p2, ma, mid, x1, x8, wf, be1, weave,
+           sc0, sc1, sc2, sc3, sc4, sc5, sc6, sc7, sc8, rc0, rc1, rc2, rc3, rc4, rc5, rc6, rc7, rc8,
            w_sem, send_sem, recv_sem):
     row = lax.axis_index("row")
     col = lax.axis_index("col")
@@ -36,15 +36,15 @@
     side_up = (data, 1 - col, row - 1)
     side_down = (data, 1 - col, row + 1)
     edge = (1 - col) * (SIDE - 1)
-    send_cols = (sc0, sc1, sc2, sc3, sc4, sc5, sc6, sc7)
-    recv_cols = (rc0, rc1, rc2, rc3, rc4, rc5, rc6, rc7)
+    send_cols = (sc0, sc1, sc2, sc3, sc4, sc5, sc6, sc7, sc8)
+    recv_cols = (rc0, rc1, rc2, rc3, rc4, rc5, rc6, rc7, rc8)
 
     loads = (
-        (w8, vw8), (we1b, ve1b), (we2a, ve2a.at[:, :, 64:256, :]), (we2b, ve2b), (wma, vma), (wmb, vmb),
+        (we1b, re1b), (we2a, ve2a.at[:, :, 64:256, :]), (we2b, ve2b), (wma, vma), (wmb, vmb),
         (wu2, vu2), (wd2a, vd2a), (wd2b, vd2b), (wu1, vu1), (wd1a, vd1a), (wd1b, vd1b.at[:, :, 0:192, :]),
     )
     copies = [pltpu.make_async_copy(src, dst, w_sem.at[k]) for k, (src, dst) in enumerate(loads)]
-    for k in range(4):
+    for k in range(3):
         copies[k].start()
 
     def zero_halo(buf, factor):
@@ -52,7 +52,7 @@
         buf[0, :, ROWS - 1] = jnp.zeros(shape, BF16)
         buf[factor - 1, :, 0] = jnp.zeros(shape, BF16)
 
-    for buf, factor in ((h1, 4), (cat1, 4), (p1, 2), (e2a, 2), (cat2, 2), (p2, 1), (ma, 1)):
+    for buf, factor in ((h1, 4), (cat1, 4), (p1, 2), (e2a, 2), (cat2, 2), (p2, 1), (ma, 1), (x1, 1)):
         zero_halo(buf, factor)
 
     def zero_plane(t, carry):
@@ -78,30 +78,102 @@
         pl.semaphore_signal(barrier, inc=1, device_id=down, device_id_type=MESH)
         pl.semaphore_signal(barrier, inc=1, device_id=side_down, device_id_type=MESH)
 
-    for k in range(4, len(copies)):
+    for k in range(3, len(copies)):
         copies[k].start()
 
     def relu_bias(acc, bias):
-        return jnp.maximum(acc + bias[...], 0.0)
-
-    copies[0].wait()
-    ext = ROWS * SIDE
-    pos = lax.broadcasted_iota(jnp.int32, (ext, 256), 0)
-    pos_row = pos // SIDE
-    pos_col = lax.rem(pos, SIDE)
-    off_rows = ((pos_row == 0) & (row == 0)) | ((pos_row == ROWS - 1) & (row == last))
-    off_left = off_rows | ((pos_col == 0) & (col == 0))
-    off_right = off_rows | ((pos_col == SIDE - 1) & (col == 1))
-
-    def first_conv(a, carry):
-        for b in range(6):
-            acc = jnp.dot(x8[...], vw8[a * 6 + b], preferred_element_type=F32)
-            off = off_left if b == 0 else off_right if b == 5 else off_rows
-            out = jnp.where(off, 0.0, relu_bias(acc, be1a)).astype(BF16)
-            h1[a, b] = out.reshape(ROWS, SIDE, 256)
-        return carry
-
-    lax.fori_loop(0, 4, first_conv, 0)
+        return jnp.maximum(acc + bias[...].reshape(1, bias.shape[-1]), 0.0)
+
+    def iota(shape, dim):
+        return lax.broadcasted_iota(jnp.int32, shape, dim)
+
+    def ones_at(mask):
+        return mask.astype(F32).astype(BF16)
+
+    at, to = iota((64, 64), 0), iota((64, 64), 1)
+    split_cols = ones_at(at == lax.rem(to, 16) * 4 + to // 16)
+    at, to = iota((PIX, 64), 0), iota((PIX, 64), 1)
+    own_col = lax.rem(at, 16) == lax.rem(to, 16)
+    image = None
+    for ch in range(3):
+        cols = jnp.dot(x[ch], split_cols, preferred_element_type=F32).astype(BF16)
+        for a in range(4):
+            spread = ones_at(to == (at // 16) * 4 + a)
+            lines = jnp.where(own_col, jnp.dot(spread, cols, preferred_element_type=F32), 0.0).astype(BF16)
+            fold = ones_at(iota((64, 128), 1) == iota((64, 128), 0) // 16 + (ch * 16 + a * 4))
+            part = jnp.dot(lines, fold, preferred_element_type=F32)
+            image = part if image is None else image + part
+    x1[0, 1, 1:ROWS - 1] = image.astype(BF16).reshape(SIDE, SIDE, 128)
+
+    def first_weights():
+        wf[...] = jnp.zeros(wf.shape, F32)
+        for t in range(9):
+            wf[4 * t:4 * t + 3, 0:192] = we1a[t // 3, t % 3].astype(F32)
+        k, m = iota((PATCH, 40), 0), iota((PATCH, 40), 1)
+        base = (k // 32) * 12 + (lax.rem(k, 32) // 4) * 4 + lax.rem(k, 4)
+        row_ok = k // 32
+        col_ok = lax.rem(k, 32) // 4
+
+        def body(t, carry):
+            a, b = t // 6, lax.rem(t, 6)
+            good = (row_ok >= a) & (row_ok <= a + 2) & (col_ok >= b) & (col_ok <= b + 2)
+            place = ones_at(good & (m == base - a * 12 - b * 4))
+            vw8[t] = jnp.dot(place, wf[...].astype(BF16), preferred_element_type=F32).astype(BF16)
+            return carry
+
+        lax.fori_loop(0, 24, body, 0)
+        be1[0:1, 0:192] = be1a[...].reshape(1, 192)
+        be1[0:1, 192:256] = jnp.zeros((1, 64), F32)
+        be1[1:2, :] = jnp.concatenate([jnp.zeros((1, 64), F32), be1b[...].reshape(1, 192)], axis=1)
+        n, m = iota((PIX, PIX), 0), iota((PIX, PIX), 1)
+        weave[...] = ones_at(m == lax.rem(n, 4) * 64 + (n // 64) * 16 + lax.rem(n, 64) // 4)
+        copies[0].wait()
+
+        def shift(t, carry):
+            a, b = t // 3, lax.rem(t, 3)
+            value = re1b[a, b].astype(F32)
+            ve1b[a, b, 0:192] = jnp.concatenate([jnp.zeros((192, 64), F32), value], axis=1).astype(BF16)
+            ve1b[a, b, 192:256] = jnp.zeros((64, 256), BF16)
+            return carry
+
+        lax.fori_loop(0, 9, shift, 0)
+
+    def patch_matrix():
+        blocks = []
+        for dx in range(3):
+            plane = x1[0, dx].reshape(ROWS * SIDE, 128)
+            pad = jnp.zeros((SIDE, 128), BF16)
+            blocks.append((jnp.concatenate([pad, plane[:-SIDE]], axis=0), plane, jnp.concatenate([plane[SIDE:], pad], axis=0)))
+        total = None
+        lane, k = iota((128, PATCH), 0), iota((128, PATCH), 1)
+        ch, a, b = lane // 16, lax.rem(lane, 16) // 4, lax.rem(lane, 4)
+        for dy in range(3):
+            for dx in range(3):
+                py, px = a + (4 * dy - 3), b + (4 * dx - 2)
+                good = (ch < 3) & (py >= 0) & (py < 6) & (px >= 0) & (px < 8)
+                place = ones_at(good & (k == py * 32 + px * 4 + ch))
+                part = jnp.dot(blocks[dx][dy], place, preferred_element_type=F32)
+                total = part if total is None else total + part
+        x8[...] = total.astype(BF16)
+
+    def first_layer():
+        ext = ROWS * SIDE
+        pos = iota((ext, 256), 0)
+        pos_row = pos // SIDE
+        pos_col = lax.rem(pos, SIDE)
+        off_rows = ((pos_row == 0) & (row == 0)) | ((pos_row == ROWS - 1) & (row == last))
+        off_left = off_rows | ((pos_col == 0) & (col == 0))
+        off_right = off_rows | ((pos_col == SIDE - 1) & (col == 1))
+
+        def body(a, carry):
+            for b in range(6):
+                acc = jnp.dot(x8[...], vw8[a * 6 + b], preferred_element_type=F32)
+                off = off_left if b == 0 else off_right if b == 5 else off_rows
+                out = jnp.where(off, 0.0, jnp.maximum(acc + be1[0:1, :], 0.0)).astype(BF16)
+                h1[a, b] = out.reshape(ROWS, SIDE, 256)
+            return carry
+
+        lax.fori_loop(0, 4, body, 0)
 
     def taps(buf, factor, a):
         rows = []
@@ -173,7 +245,7 @@
         to_side_down = remote(cols.at[factor - 1], got.at[factor], 4, side_down)
         return to_side, to_up, to_down, to_side_up, to_side_down
 
-    def exchange(index, buf):
+    def exchange(index, buf, meanwhile=None):
         factor = EXCHANGE_FACTOR[index]
         lanes = EXCHANGE_LANES[index]
         cols, got = send_cols[index], recv_cols[index]
@@ -197,6 +269,9 @@
             plane = buf[a, 1 + (factor - 1) * (1 - col), 1:ROWS - 1].reshape(PIX, lanes)
             cols[a] = jnp.dot(pick, plane, preferred_element_type=F32).astype(BF16)
         to_side, to_up, to_down, to_side_up, to_side_down = messages(index, buf)
+        if index == 8:
+            total = jnp.where(has_up, 2, 0) + jnp.where(has_down, 2, 0) + 1
+            pl.semaphore_wait(barrier, total)
         to_side.start()
 
         @pl.when(has_up)
@@ -209,6 +284,8 @@
             to_down.start()
             to_side_down.start()
 
+        if meanwhile is not None:
+            meanwhile()
         to_side.wait()
 
         @pl.when(has_up)
@@ -240,42 +317,41 @@
 
         lax.fori_loop(0, factor, insert, 0)
 
+    exchange(8, x1, first_weights)
+    patch_matrix()
+    first_layer()
+    conv_layer(h1, cat1, 4, ve1b, be1.at[1:2], 128)
+    pool(cat1, p1, 2, 128, 256)
+    exchange(0, p1)
     copies[1].wait()
-    conv_layer(h1, cat1, 4, ve1b, be1b, 128)
-    pool(cat1, p1, 2, 128, 256)
-
-    total = jnp.where(has_up, 2, 0) + jnp.where(has_down, 2, 0) + 1
-    pl.semaphore_wait(barrier, total)
-    exchange(0, p1)
-    copies[2].wait()
     conv_layer(p1, e2a, 2, ve2a, be2a, 0)
     exchange(1, e2a)
-    copies[3].wait()
+    copies[2].wait()
     conv_layer(e2a, cat2, 2, ve2b, be2b, 384)
     pool(cat2, p2, 1, 384, 384)
     exchange(2, p2)
-    copies[4].wait()
+    copies[3].wait()
     conv_layer(p2, ma, 1, vma, bma, 0)
     exchange(3, ma)
+    copies[4].wait()
+    mid[...] = conv(ma, 1, 0, vmb, bmb)
     copies[5].wait()
-    mid[...] = conv(ma, 1, 0, vmb, bmb)
-    copies[6].wait()
     for p in range(2):
         for q in range(2):
             out = jnp.dot(mid[...], vu2[p, q], preferred_element_type=F32).astype(BF16)
             cat2[p, q + 1, 1:ROWS - 1, :, 0:384] = out.reshape(SIDE, SIDE, 384)
     exchange(4, cat2)
-    copies[7].wait()
+    copies[6].wait()
     conv_layer(cat2, e2a, 2, vd2a, bd2a, 0)
     exchange(5, e2a)
-    copies[8].wait()
+    copies[7].wait()
 
     def dec2b(a, carry):
         d2[pl.ds(2 * a * PIX, 2 * PIX)] = conv(e2a, 2, a, vd2b, bd2b)
         return carry
 
     lax.fori_loop(0, 2, dec2b, 0)
-    copies[9].wait()
+    copies[8].wait()
 
     def up1(t, carry):
         a = t // 2
@@ -289,16 +365,23 @@
 
     lax.fori_loop(0, 4, up1, 0)
     exchange(6, cat1)
-    copies[10].wait()
+    copies[9].wait()
     conv_layer(cat1, d1a, 4, vd1a, bd1a, 0, transposed=True)
     exchange(7, d1a)
-    copies[11].wait()
+    copies[10].wait()
+
+    head_bias = jnp.zeros((6, 64), F32)
+    for c in range(6):
+        head_bias = jnp.where(iota((6, 64), 0) == c, bh[c], head_bias)
 
     def dec1b(a, carry):
         out = conv(d1a, 4, a, vd1b, bd1b)
-        for b in range(4):
-            head = lax.dot_general(wh[...], out[b * PIX:(b + 1) * PIX], (((1,), (1,)), ((), ())), preferred_element_type=F32)
-            y[a, b] = head + bh[...]
+        for g in range(4):
+            picked = jnp.concatenate([out[b * PIX + g * 64:b * PIX + g * 64 + 64] for b in range(4)], axis=0)
+            lines = jnp.dot(weave[...], picked, preferred_element_type=F32).astype(BF16)
+            head = lax.dot_general(wh[...], lines, (((1,), (1,)), ((), ())), preferred_element_type=F32)
+            for i in range(4):
+                y[4 * (4 * g + i) + a] = head[:, i * 64:i * 64 + 64] + head_bias
         return carry
 
     lax.fori_loop(0, 4, dec1b, 0)
@@ -306,39 +389,7 @@
 
 def solution(mesh):
     row_count = mesh.shape["row"]
-    col_count = mesh.shape["col"]
-    row_next = [(source, source + 1) for source in range(row_count - 1)]
-    row_prev = [(source + 1, source) for source in range(row_count - 1)]
-    col_next = [(source, source + 1) for source in range(col_count - 1)]
-    col_prev = [(source + 1, source) for source in range(col_count - 1)]
     tile_spec = P(("data", "row"), "col", None)
-
-    def with_halo(tile, depth):
-        from_above = lax.ppermute(tile[-depth:], "row", row_next)
-        from_below = lax.ppermute(tile[:depth], "row", row_prev)
-        tall_tile = jnp.concatenate([from_above, tile, from_below], axis=0)
-        from_left = lax.ppermute(tall_tile[:, -depth:], "col", col_next)
-        from_right = lax.ppermute(tall_tile[:, :depth], "col", col_prev)
-        return jnp.concatenate([from_left, tall_tile, from_right], axis=1)
-
-    def patches(image_tile):
-        haloed = with_halo(image_tile, 2)
-        padded = jnp.pad(haloed, ((3, 5), (0, 0), (0, 0)))
-        select = np.zeros((68, 8, 16), np.float32)
-        for px in range(8):
-            for j in range(16):
-                select[4 * j + px, px, j] = 1.0
-        picked = jnp.einsum("rwc,wpj->rpjc", padded, jnp.asarray(select, BF16), preferred_element_type=F32).astype(BF16)
-        blocks = picked.reshape(19, 4, 8, 16, 3)
-        rows = jnp.concatenate([blocks[:18], blocks[1:, :2]], axis=1)
-        return rows.transpose(0, 3, 1, 2, 4).reshape(288, 144)
-
-    def first_weights(w_enc1a):
-        planes = []
-        for a in range(4):
-            for b in range(6):
-                planes.append(jnp.pad(w_enc1a, ((a, 3 - a), (b, 5 - b), (0, 0), (0, 64))))
-        return jnp.stack(planes).reshape(24, 144, 256)
 
     def device_body(image_tile, *params):
         (w_enc1a, b_enc1a, w_enc1b, b_enc1b, w_enc2a, b_enc2a, w_enc2b, b_enc2b,
@@ -347,36 +398,35 @@
         anywhere = pl.BlockSpec(memory_space=pl.ANY)
         vmem = pl.BlockSpec(memory_space=pltpu.VMEM)
         operands = [
-            patches(image_tile), first_weights(w_enc1a),
-            jnp.pad(w_enc1b, ((0, 0), (0, 0), (0, 64), (64, 0))), w_enc2a, w_enc2b, w_mid_a, w_mid_b,
+            jnp.transpose(image_tile, (2, 0, 1)), w_enc1a, w_enc1b, w_enc2a, w_enc2b, w_mid_a, w_mid_b,
             w_up2, w_dec2a, w_dec2b, jnp.swapaxes(w_up1, 2, 3), jnp.swapaxes(w_dec1a, 2, 3), w_dec1b, w_head.T,
-            jnp.pad(b_enc1a, (0, 64))[None], jnp.pad(b_enc1b, (64, 0))[None], b_enc2a[None], b_enc2b[None],
-            b_mid_a[None], b_mid_b[None], b_dec2a[None], b_dec2b[None], b_dec1a[None], b_dec1b[None], b_head[:, None],
+            b_enc1a, b_enc1b, b_enc2a, b_enc2b, b_mid_a, b_mid_b, b_dec2a, b_dec2b, b_dec1a, b_dec1b, b_head,
         ]
-        specs = [vmem] + [anywhere] * 12 + [vmem] * 12
+        specs = [vmem] * 2 + [anywhere] * 11 + [vmem] * 11 + [pl.BlockSpec(memory_space=pltpu.SMEM)]
         level = lambda factor, lanes: pltpu.VMEM((factor, factor + 2, ROWS, SIDE, lanes), BF16)
         scratch = [
-            pltpu.VMEM((24, 144, 256), BF16), pltpu.VMEM((3, 3, 256, 256), BF16), pltpu.VMEM((3, 3, 256, 384), BF16),
+            pltpu.VMEM((24, PATCH, 256), BF16), pltpu.VMEM((3, 3, 192, 192), BF16), pltpu.VMEM((3, 3, 256, 256), BF16), pltpu.VMEM((3, 3, 256, 384), BF16),
             pltpu.VMEM((3, 3, 384, 384), BF16), pltpu.VMEM((3, 3, 384, 768), BF16), pltpu.VMEM((3, 3, 768, 768), BF16),
             pltpu.VMEM((2, 2, 768, 384), BF16), pltpu.VMEM((3, 3, 768, 384), BF16), pltpu.VMEM((3, 3, 384, 384), BF16),
             pltpu.VMEM((2, 2, 192, 384), BF16), pltpu.VMEM((3, 3, 192, 384), BF16), pltpu.VMEM((3, 3, 256, 192), BF16),
             level(4, 256), level(4, 384), level(4, 256), level(2, 256), level(2, 384), level(2, 768),
             pltpu.VMEM((4 * PIX, 384), BF16), level(1, 384), level(1, 768), pltpu.VMEM((PIX, 768), BF16),
+            level(1, 128), pltpu.VMEM((ROWS * SIDE, PATCH), BF16), pltpu.VMEM((40, 256), F32), pltpu.VMEM((2, 256), F32),
+            pltpu.VMEM((PIX, PIX), BF16),
         ]
         scratch += [pltpu.VMEM((f, SIDE, c), BF16) for f, c in zip(EXCHANGE_FACTOR, EXCHANGE_LANES)]
         scratch += [pltpu.VMEM((f + 2, SIDE, c), BF16) for f, c in zip(EXCHANGE_FACTOR, EXCHANGE_LANES)]
-        scratch += [pltpu.SemaphoreType.DMA((12,)), pltpu.SemaphoreType.DMA((8, 5)), pltpu.SemaphoreType.DMA((8, 5))]
+        scratch += [pltpu.SemaphoreType.DMA((11,)), pltpu.SemaphoreType.DMA((9, 5)), pltpu.SemaphoreType.DMA((9, 5))]
         out = pl.pallas_call(
             functools.partial(kernel, row_count),
             name="unet",
-            out_shape=jax.ShapeDtypeStruct((4, 4, 6, PIX), F32),
+            out_shape=jax.ShapeDtypeStruct((64, 6, 64), F32),
             in_specs=specs,
             out_specs=vmem,
             scratch_shapes=scratch,
             compiler_params=pltpu.CompilerParams(collective_id=0, has_side_effects=True, vmem_limit_bytes=67043328),
         )(*operands)
-        grid = out.reshape(4, 4, 6, 16, 16).transpose(3, 0, 4, 1, 2)
-        return grid.reshape(64, 64, 6)
+        return jnp.transpose(out, (0, 2, 1))
 
     def program(image, *params):
         mapped = jax.shard_map(device_body, mesh=mesh, in_specs=(tile_spec,) + tuple([P()] * len(params)), out_specs=tile_spec, check_vma=False)

time: 159 us -> 105 us (0.66)
  local copies, waits for them, and re-layouts: 51.7 us -> 1.67 us
  starting transfers between devices: 10.2 us -> 0 us
  Pallas kernels: 93.5 us -> 103 us
    another operation x25 -> x0, local copies, waits for them, and re-layouts: 13.6 us -> none  [first_weights(): return jnp.stack(planes).reshape(24, 144, 256)]
    unnamed x40 -> x0, local copies, waits for them, and re-layouts: 11.1 us -> none
    ppermute x4 -> x0, starting transfers between devices: 10.2 us -> none  [the longest x1 4.24 us: with_halo(): from_left = lax.ppermute(tall_tile[:, -depth:], 'col', col_next)]
    pallas_call x1, Pallas kernels: 93.5 us -> 103 us  [device_body(): pl.pallas_call(functools.partial(kernel, row_count), name='unet', out_sha...]
    pad x6 -> x0, local copies, waits for them, and re-layouts: 8.86 us -> none  [the longest x3 4.86 us: first_weights(): planes.append(jnp.pad(w_enc1a, ((a, 3 - a), (b, 5 - b), (0, 0), (0, 64))))]
    broadcast_in_dim x7 -> x0, local copies, waits for them, and re-layouts: 6.22 us -> none  [the longest x1 1.33 us: device_body(): b_head[:, None]]
    reshape x4 -> x0, local copies, waits for them, and re-layouts: 4.62 us -> none  [the longest x1 2.14 us: device_body(): return grid.reshape(64, 64, 6)]
    slice x5 -> x0, local copies, waits for them, and re-layouts: 2.5 us -> none  [the longest x2 1.46 us: with_halo(): from_above = lax.ppermute(tile[-depth:], 'row', row_next)]
  transfers between devices with their start and end apart: 4 -> 0, of which waited for: 0 -> 0; matrix products, arithmetic and copies ran while one was open for 26% -> 0% of each run, Pallas kernels for 0% -> 0%
where the time goes in v1:
time: 105 us; the launch traced here: 104 us
  Pallas kernels  103 us (98%)
  local copies, waits for them, and re-layouts  1.67 us (2%)
    pallas_call x1, Pallas kernels, device_body(): pl.pallas_call(functools.partial(kernel, row_count), name='unet', out_sha...  103 us

profile of v1, /device:TPU:0, one launch (start us, length us, event | category | flops | bytes accessed | tf_op | source)
XLA Modules:
  0.0 104.5 jit_solution(11694210953239132488)
XLA Ops:
  0.0 102.8 %unet.1 = f32[64,6,64]{2,1,0:T(8,128)} custom-call(bf16[3,64,64]{2,1,0:T(8,128)(2,1)} %bitcast.8, bf16[3,3,3,192]{3,2,1,0:T(4,128)(2,1)} %we1a.1, bf16[3,3,192,192]{3,2,1,0:T(8,128)(2,1)} %we1b.1, bf16[3,3,192,384]{3,2,1,0:T(8,128)(2,1)} %we2a.1, bf16[3,3,384,384]{3,2,1,0:T(8,128)(2,1)} %we2b.1, bf16[3,3,384,768]{3,2,1,0:T(8,128)(2,1)} %wma.1, ...), custom_call_target="tpu_custom_call" | custom-call | tf_op jit(solution)/shard_map/unet/pallas_call | solution.py:420
  102.8 1.7 %copy.26 = f32[64,64,6]{1,0,2:T(8,128)} copy(f32[64,64,6]{1,2,0:T(8,128)} %bitcast.6) | data formatting | bytes 196608 | tf_op jit(solution)/shard_map/transpose | solution.py:429
